TPU v7x, 32 devices: a whole 2x2x4 slice. The times are simulated.
32 devices in a mesh: row: 4 (over z), col: 8 (over y, x, core).
Axes of the slice: x: 2, y: 2, z: 4, core: 2. Of those that a mesh axis runs over, the one named last changes fastest.
Arguments:
- grad: float32 [8192, 14336], P(('row', 'col')), may hold values from -30 to 30
- momentum: float32 [8192, 14336], P(('row', 'col')), may hold values from -6 to 6
- weight: float32 [8192, 14336], P(('row', 'col')), may hold values from -0.75 to 0.75
Outputs:
- new_weight: float32 [8192, 14336], P('row', 'col')
- new_momentum: float32 [8192, 14336], P('row', 'col')
All inputs are finite; a program needn't handle non-finite values.
Results may differ from a plain program's by a relative error of at most 0.00002.
Values sent between devices are 32-bit elements; how exact they have to be, the bound alone decides.
No kernel may reach another device: no remote copies, remote signals or barrier semaphores. Data moves between devices by JAX's collectives and lax.ppermute only.
A program may use at most 192 MiB of HBM per device.

v0:
```python
import functools
import math

import jax
import jax.numpy as jnp
from jax import lax
from jax.experimental import pallas as pl
from jax.experimental.pallas import tpu as pltpu
from jax.sharding import PartitionSpec as P


F32 = jnp.float32
LANES = 128


def hop(x, axis, k, n):
    return lax.ppermute(x, axis, [(i, i ^ k) for i in range(n)])


def cost(passes, rows, cols):
    return pl.CostEstimate(flops=4 * rows * cols, bytes_accessed=4 * passes * rows * cols, transcendentals=0)


PARAMS = pltpu.CompilerParams(vmem_limit_bytes=67043328)


def block_rows(rows, start, most=256):
    b = most
    while rows % b or start % b:
        b //= 2
    return b


def copy_kernel(at, x_ref, o_ref):
    o_ref[...] = x_ref[...]


def cut(x, at, cols, start, rows):
    b = block_rows(rows, start)
    s = start // b
    return pl.pallas_call(
        copy_kernel,
        grid_spec=pltpu.PrefetchScalarGridSpec(
            num_scalar_prefetch=1, grid=(rows // b,),
            in_specs=[pl.BlockSpec((b, cols), lambda i, at: (s + i, at[0]))],
            out_specs=pl.BlockSpec((b, cols), lambda i, at: (i, 0))),
        out_shape=jax.ShapeDtypeStruct((rows, cols), F32),
        cost_estimate=cost(2, rows, cols), name="cut", compiler_params=PARAMS,
    )(at, x)


def calc_kernel(at, factor, m_ref, g_ref, o_ref):
    o_ref[...] = F32(0.9) * m_ref[...] + factor[0] * g_ref[...]


def calc(m, g, factor, at, cols, start, rows):
    b = block_rows(rows, start)
    s = start // b
    spec = pl.BlockSpec((b, cols), lambda i, at: (s + i, at[0]))
    return pl.pallas_call(
        calc_kernel,
        grid_spec=pltpu.PrefetchScalarGridSpec(
            num_scalar_prefetch=1, grid=(rows // b,),
            in_specs=[pl.BlockSpec(memory_space=pltpu.SMEM), spec, spec],
            out_specs=pl.BlockSpec((b, cols), lambda i, at: (i, 0))),
        out_shape=jax.ShapeDtypeStruct((rows, cols), F32),
        cost_estimate=cost(3, rows, cols), name="calc", compiler_params=PARAMS,
    )(at, factor, m, g)


def finish_kernel(parts, at, *refs):
    nw_ref, nm_ref = refs[-2:]
    for q in range(parts):
        @pl.when(pl.program_id(0) == q)
        def _():
            m = refs[2 * q + 1][...]
            nm_ref[...] = m
            nw_ref[...] = refs[2 * q][...] - F32(0.1) * m


def finish(at, pairs, outs, shape, piece, start, rows, within):
    cols = shape[1]
    b = block_rows(rows, start)
    s, p, o = start // b, piece // b, within // b
    parts = len(pairs)
    last = rows // b - 1

    def spec(part, first):
        def index(q, i, at):
            turn = jnp.where(q == part, i, jnp.where(q < part, 0, last))
            return (first + turn, 0)

        return pl.BlockSpec((b, cols), index if parts > 1 else lambda q, i, at: (first + i, 0))

    ospec = pl.BlockSpec((b, cols), lambda q, i, at: (at[q] * p + s + i, 0))
    hbm = pl.BlockSpec(memory_space=pl.ANY)
    return pl.pallas_call(
        functools.partial(finish_kernel, parts),
        grid_spec=pltpu.PrefetchScalarGridSpec(
            num_scalar_prefetch=1, grid=(parts, rows // b),
            in_specs=[spec(part, first) for part in range(parts) for first in (o, 0)] + [hbm] * 2, out_specs=[ospec, ospec]),
        out_shape=[jax.ShapeDtypeStruct(shape, F32)] * 2,
        input_output_aliases={2 * parts + 1: 0, 2 * parts + 2: 1},
        cost_estimate=cost(4 * parts, rows, cols), name="finish", compiler_params=PARAMS,
    )(at, *[x for pair in pairs for x in pair], *outs)


def own_kernel(at, factor, w_ref, m_ref, g_ref, nw_ref, nm_ref):
    m = F32(0.9) * m_ref[...] + factor[0] * g_ref[...]
    nm_ref[...] = m
    nw_ref[...] = w_ref[...] - F32(0.1) * m


def own(at, factor, w, m, g, n):
    rows, cols = w.shape[0], w.shape[1] // n
    b = block_rows(rows, 0)
    t = rows // b
    spec = pl.BlockSpec((b, cols), lambda i, at: (i, at[0]))
    ospec = pl.BlockSpec((b, cols), lambda i, at: (at[0] * t + i, 0))
    return pl.pallas_call(
        own_kernel,
        grid_spec=pltpu.PrefetchScalarGridSpec(
            num_scalar_prefetch=1, grid=(t,),
            in_specs=[pl.BlockSpec(memory_space=pltpu.SMEM)] + [spec] * 3, out_specs=[ospec, ospec]),
        out_shape=[jax.ShapeDtypeStruct((rows * n, cols), F32)] * 2,
        cost_estimate=cost(5, rows, cols), name="own", compiler_params=PARAMS,
    )(at, factor, w, m, g)


def squares_kernel(g_ref, o_ref, acc_ref):
    i = pl.program_id(0)
    rows, ff = g_ref.shape

    @pl.when(i == 0)
    def _():
        acc_ref[...] = jnp.zeros_like(acc_ref)

    for c in range(0, ff, LANES):
        g = g_ref[:, c:c + LANES]
        acc_ref[:, c:c + LANES] += jnp.sum((g * g).reshape(rows // 8, 8, LANES), axis=0)

    @pl.when(i == pl.num_programs(0) - 1)
    def _():
        parts = [acc_ref[:, c:c + LANES] for c in range(0, ff, LANES)]
        while len(parts) > 1:
            parts = [sum(parts[j:j + 2]) for j in range(0, len(parts), 2)]
        o_ref[...] = parts[0]


def squares(g):
    rows, ff = g.shape
    b = block_rows(rows, 0, 32)
    return pl.pallas_call(
        squares_kernel,
        grid=(rows // b,),
        in_specs=[pl.BlockSpec((b, ff), lambda i: (i, 0))],
        out_specs=pl.BlockSpec((8, LANES), lambda i: (0, 0)),
        out_shape=jax.ShapeDtypeStruct((8, LANES), F32),
        scratch_shapes=[pltpu.VMEM((8, ff), F32)],
        cost_estimate=cost(1, rows, ff), name="squares", compiler_params=PARAMS,
    )(g)


def last_pair(n):
    return [k for k in (4, 2) if k < n]


def w_parcels(k, n, rows):
    e = rows // 8
    if e % 8 == 0 and k == n - 1:
        return [(0, e), (e, 3 * e), (4 * e, 4 * e)]
    return [(0, rows)]


SPLIT = lambda e: [(0, 4 * e), (4 * e, 2 * e), (6 * e, e), (7 * e, e)]


def m_parcels(k, n, rows):
    e = rows // 8
    if e % 8 == 0 and k in last_pair(n):
        return SPLIT(e)
    return w_parcels(k, n, rows)


def plan(n):
    far = list(range(n - 1, 3, -1))
    near = [k for k in (3, 2, 1) if k < n]
    return far, near


def body(limit, n, nrow, grad, momentum, weight):
    me = lax.axis_index("col")
    rows, ff = weight.shape
    cols = ff // n
    far, near = plan(n)
    at = {k: jnp.reshape(me ^ k, (1,)).astype(jnp.int32) for k in range(n)}
    moved_w, moved_m = {}, {}

    def send_w(k):
        for j, (s, r) in enumerate(w_parcels(k, n, rows)):
            moved_w[k, j] = hop(cut(weight, at[k], cols, s, r), "col", k, n)

    for k in far + near:
        send_w(k)
    part = squares(grad)
    bits = rounds(n, nrow)
    for axis, k, size in bits:
        part = part + hop(part, axis, k, size)
    total = jnp.sum(part)
    factor = jnp.reshape(jnp.minimum(F32(1.0), limit / (jnp.sqrt(total) + F32(1e-06))), (1,))
    for k in far + near:
        for j, (s, r) in enumerate(m_parcels(k, n, rows)):
            moved_m[k, j] = hop(calc(momentum, grad, factor, at[k], cols, s, r), "col", k, n)
    outs = own(at[0], factor, weight, momentum, grad, n)
    for group in finish_order(n, rows):
        (s, r) = m_parcels(group[0][0], n, rows)[group[0][1]]
        pairs, where = [], []
        for k, j in group:
            i = max(i for i, (ws, _) in enumerate(w_parcels(k, n, rows)) if ws <= s)
            pairs.append((moved_w[k, i], moved_m[k, j]))
            where.append(at[k])
        within = s - w_parcels(group[0][0], n, rows)[i][0]
        outs = finish(jnp.concatenate(where), pairs, outs, (rows * n, cols), rows, s, r, within)
    return tuple(outs)


def finish_order(n, rows):
    end = last_pair(n)
    order = [1] + [k for k in range(n - 1, 1, -1) if k not in end]
    groups = [[(k, j)] for k in order for j in range(len(m_parcels(k, n, rows)))]
    for j in range(len(m_parcels(end[0], n, rows))):
        groups.append([(k, j) for k in end])
    return groups


def rounds(n, nrow):
    col = [("col", 1 << j, n) for j in range(n.bit_length() - 1)]
    row = [("row", 1 << j, nrow) for j in range(nrow.bit_length() - 1)]
    return col[2:] + col[:1] + row + col[1:2]


def solution(mesh):
    spec = P(("row", "col"), None)
    n, nrow = mesh.shape["col"], mesh.shape["row"]

    def run(grad, momentum, weight):
        limit = F32(math.sqrt(grad.shape[0] * grad.shape[1]))
        f = jax.shard_map(lambda g, m, w: body(limit, n, nrow, g, m, w), mesh=mesh, in_specs=(spec,) * 3, out_specs=(P("row", "col"),) * 2, check_vma=False)
        return f(grad, momentum, weight)

    return run
```

profile of v0, /device:TPU:0, one launch (start us, length us, event | category | flops | bytes accessed | tf_op | source)
XLA Modules:
  0.0 372.1 jit_solution(2463057888246174514)
XLA Ops:
  3.4 3.4 collective-permute-start.23
  6.8 8.0 %squares.1 = f32[8,128]{1,0:T(8,128)} custom-call(f32[256,14336]{1,0:T(8,128)} %g_ref.33), custom_call_target="tpu_custom_call" | custom-call | flops 14680064 | bytes 14680064 | tf_op jit(solution)/shard_map/squares/pallas_call | solution.py:153
  15.4 3.9 %collective-permute-done.1 = f32[8,128]{1,0:T(8,128)S(1)} collective-permute-done((f32[8,128]{1,0:T(8,128)}, f32[8,128]{1,0:T(8,128)S(1)}, u32[]{:S(2)}, u32[]{:S(2)}) %collective-permute-start.1) | collective-permute-done | bytes 4128 | tf_op jit(solution)/shard_map/ppermute | solution.py:17
  29.7 3.1 collective-permute-done.5
  44.9 3.0 calc.27
  58.1 53.4 %collective-permute-done.11.refs_1_ = f32[64,1792]{1,0:T(8,128)} collective-permute-done((f32[64,1792]{1,0:T(8,128)}, f32[64,1792]{1,0:T(8,128)}, u32[]{:S(2)}, u32[]{:S(2)}) %collective-permute-start.11) | collective-permute-done | bytes 458784 | tf_op jit(solution)/shard_map/ppermute | solution.py:17
  122.7 3.0 cut.12
  136.6 3.6 calc.29
  140.2 3.5 calc.25
  143.7 3.5 calc.24
  147.2 22.6 %collective-permute-done.19.refs_0_ = f32[256,1792]{1,0:T(8,128)} collective-permute-done((f32[256,1792]{1,0:T(8,128)}, f32[256,1792]{1,0:T(8,128)}, u32[]{:S(2)}, u32[]{:S(2)}) %collective-permute-start.19) | collective-permute-done | bytes 1835040 | tf_op jit(solution)/shard_map/ppermute | solution.py:17
  169.8 38.8 %collective-permute-done.17.refs_0_ = f32[256,1792]{1,0:T(8,128)} collective-permute-done((f32[256,1792]{1,0:T(8,128)}, f32[256,1792]{1,0:T(8,128)}, u32[]{:S(2)}, u32[]{:S(2)}) %collective-permute-start.17) | collective-permute-done | bytes 1835040 | tf_op jit(solution)/shard_map/ppermute | solution.py:17
  209.9 3.5 calc.23
  213.7 34.8 %collective-permute-done.refs_0_ = f32[256,1792]{1,0:T(8,128)} collective-permute-done((f32[256,1792]{1,0:T(8,128)}, f32[256,1792]{1,0:T(8,128)}, u32[]{:S(2)}, u32[]{:S(2)}) %collective-permute-start) | collective-permute-done | bytes 1835040 | tf_op jit(solution)/shard_map/ppermute | solution.py:17
  256.0 31.8 %collective-permute-done.20.refs_1_ = f32[256,1792]{1,0:T(8,128)} collective-permute-done((f32[256,1792]{1,0:T(8,128)}, f32[256,1792]{1,0:T(8,128)}, u32[]{:S(2)}, u32[]{:S(2)}) %collective-permute-start.20) | collective-permute-done | bytes 1835040 | tf_op jit(solution)/shard_map/ppermute | solution.py:17
  293.2 33.4 %collective-permute-done.18.refs_1_ = f32[256,1792]{1,0:T(8,128)} collective-permute-done((f32[256,1792]{1,0:T(8,128)}, f32[256,1792]{1,0:T(8,128)}, u32[]{:S(2)}, u32[]{:S(2)}) %collective-permute-start.18) | collective-permute-done | bytes 1835040 | tf_op jit(solution)/shard_map/ppermute | solution.py:17
  329.0 4.7 %own.1 = (f32[2048,1792]{1,0:T(8,128)}, f32[2048,1792]{1,0:T(8,128)}) custom-call(s32[1]{0:T(128)} %bitcast.8.at, f32[1]{0:T(128)} %bitcast.2.factor, f32[256,14336]{1,0:T(8,128)} %w_ref.1, f32[256,14336]{1,0:T(8,128)} %m_ref.31, f32[256,14336]{1,0:T(8,128)} %g_ref.33), custom_call_target="tpu_custom_call" | custom-call | flops 1835008 | bytes 9175040 | tf_op jit(solution)/shard_map/own/pallas_call | solution.py:120
  333.7 4.1 %finish.11 = (f32[2048,1792]{1,0:T(8,128)}, f32[2048,1792]{1,0:T(8,128)}) custom-call(s32[1]{0:T(128)} %bitcast.7.at, f32[256,1792]{1,0:T(8,128)} %collective-permute-done.27.refs_0_, f32[256,1792]{1,0:T(8,128)} %collective-permute-done.28.refs_1_, f32[2048,1792]{1,0:T(8,128)} %get-tuple-element.24.refs_2_, ...), custom_call_target="tpu_custom_call", output_to_operand_aliasing={{0}: (3, {}), {1}: (4, {})} | custom-call | flops 1835008 | bytes 7340032 | tf_op jit(solution)/shard_map/finish/pallas_call | solution.py:97
  339.6 3.3 finish.13
  345.7 4.1 %finish.15 = (f32[2048,1792]{1,0:T(8,128)}, f32[2048,1792]{1,0:T(8,128)}) custom-call(s32[1]{0:T(128)} %bitcast.5.at, f32[256,1792]{1,0:T(8,128)} %collective-permute-done.19.refs_0_, f32[256,1792]{1,0:T(8,128)} %collective-permute-done.20.refs_1_, f32[2048,1792]{1,0:T(8,128)} %get-tuple-element.32.refs_2_, ...), custom_call_target="tpu_custom_call", output_to_operand_aliasing={{0}: (3, {}), {1}: (4, {})} | custom-call | flops 1835008 | bytes 7340032 | tf_op jit(solution)/shard_map/finish/pallas_call | solution.py:97
  349.8 4.1 %finish.16 = (f32[2048,1792]{1,0:T(8,128)}, f32[2048,1792]{1,0:T(8,128)}) custom-call(s32[1]{0:T(128)} %bitcast.4.at, f32[256,1792]{1,0:T(8,128)} %collective-permute-done.17.refs_0_, f32[256,1792]{1,0:T(8,128)} %collective-permute-done.18.refs_1_, f32[2048,1792]{1,0:T(8,128)} %get-tuple-element.34.refs_2_, ...), custom_call_target="tpu_custom_call", output_to_operand_aliasing={{0}: (3, {}), {1}: (4, {})} | custom-call | flops 1835008 | bytes 7340032 | tf_op jit(solution)/shard_map/finish/pallas_call | solution.py:97
  353.9 4.1 %finish.17 = (f32[2048,1792]{1,0:T(8,128)}, f32[2048,1792]{1,0:T(8,128)}) custom-call(s32[1]{0:T(128)} %bitcast.3.at, f32[256,1792]{1,0:T(8,128)} %collective-permute-done.15.refs_0_, f32[256,1792]{1,0:T(8,128)} %collective-permute-done.16.refs_1_, f32[2048,1792]{1,0:T(8,128)} %get-tuple-element.36.refs_2_, ...), custom_call_target="tpu_custom_call", output_to_operand_aliasing={{0}: (3, {}), {1}: (4, {})} | custom-call | flops 1835008 | bytes 7340032 | tf_op jit(solution)/shard_map/finish/pallas_call | solution.py:97
  358.0 4.7 %finish.18 = (f32[2048,1792]{1,0:T(8,128)}, f32[2048,1792]{1,0:T(8,128)}) custom-call(s32[2]{0:T(128)} %pad_add_fusion.at, f32[256,1792]{1,0:T(8,128)} %collective-permute-done.refs_0_, f32[128,1792]{1,0:T(8,128)} %collective-permute-done.13.refs_1_, f32[256,1792]{1,0:T(8,128)} %collective-permute-done.7.refs_2_, ...), custom_call_target="tpu_custom_call", output_to_operand_aliasing={{0}: (5, {}), {1}: (6, {})} | custom-call | flops 917504 | bytes 7340032 | tf_op jit(solution)/shard_map/finish/pallas_call | solution.py:97
  362.8 3.4 finish.19
  (77 shorter events, 85.0 us)
Async XLA Ops:
  3.4 108.0 %collective-permute-start.23 = (f32[96,1792]{1,0:T(8,128)}, f32[96,1792]{1,0:T(8,128)}, u32[]{:S(2)}, u32[]{:S(2)}) collective-permute-start(f32[96,1792]{1,0:T(8,128)} %cut.15), channel_id=1, source_target_pairs={{0,7},{1,6},{2,5},{3,4},{4,3},{5,2},{6,1},{7,0},{8,15},{9,14},{10,... | collective-permute-start | bytes 2064392 | tf_op jit(solution)/shard_map/ppermute | solution.py:17
  36.1 75.3 %collective-permute-start.11 = (f32[64,1792]{1,0:T(8,128)}, f32[64,1792]{1,0:T(8,128)}, u32[]{:S(2)}, u32[]{:S(2)}) collective-permute-start(f32[64,1792]{1,0:T(8,128)} %calc.19), channel_id=1, source_target_pairs={{0,4},{1,5},{2,6},{3,7},{4,0},{5,1},{6,2},{7,3},{8,12},{9,13},{10,... | collective-permute-start | bytes 1376264 | tf_op jit(solution)/shard_map/ppermute | solution.py:17
  38.3 12.1 %collective-permute-start.25 = (f32[32,1792]{1,0:T(8,128)}, f32[32,1792]{1,0:T(8,128)}, u32[]{:S(2)}, u32[]{:S(2)}) collective-permute-start(f32[32,1792]{1,0:T(8,128)} %cut.16), channel_id=1, source_target_pairs={{0,7},{1,6},{2,5},{3,4},{4,3},{5,2},{6,1},{7,0},{8,15},{9,14},{10,... | collective-permute-start | bytes 688136 | tf_op jit(solution)/shard_map/ppermute | solution.py:17
  40.1 13.0 %collective-permute-start.26 = (f32[32,1792]{1,0:T(8,128)}, f32[32,1792]{1,0:T(8,128)}, u32[]{:S(2)}, u32[]{:S(2)}) collective-permute-start(f32[32,1792]{1,0:T(8,128)} %calc.28), channel_id=1, source_target_pairs={{0,7},{1,6},{2,5},{3,4},{4,3},{5,2},{6,1},{7,0},{8,15},{9,14},{10,... | collective-permute-start | bytes 688136 | tf_op jit(solution)/shard_map/ppermute | solution.py:17
  44.9 80.8 %collective-permute-start.21 = (f32[128,1792]{1,0:T(8,128)}, f32[128,1792]{1,0:T(8,128)}, u32[]{:S(2)}, u32[]{:S(2)}) collective-permute-start(f32[128,1792]{1,0:T(8,128)} %cut.14), channel_id=1, source_target_pairs={{0,7},{1,6},{2,5},{3,4},{4,3},{5,2},{6,1},{7,0},{8,15},{9,14},{10,... | collective-permute-start | bytes 2752520 | tf_op jit(solution)/shard_map/ppermute | solution.py:17
  50.4 66.6 %collective-permute-start.24 = (f32[96,1792]{1,0:T(8,128)}, f32[96,1792]{1,0:T(8,128)}, u32[]{:S(2)}, u32[]{:S(2)}) collective-permute-start(f32[96,1792]{1,0:T(8,128)} %calc.27), channel_id=1, source_target_pairs={{0,7},{1,6},{2,5},{3,4},{4,3},{5,2},{6,1},{7,0},{8,15},{9,14},{10,... | collective-permute-start | bytes 2064392 | tf_op jit(solution)/shard_map/ppermute | solution.py:17
  53.1 73.9 %collective-permute-start.22 = (f32[128,1792]{1,0:T(8,128)}, f32[128,1792]{1,0:T(8,128)}, u32[]{:S(2)}, u32[]{:S(2)}) collective-permute-start(f32[128,1792]{1,0:T(8,128)} %calc.26), channel_id=1, source_target_pairs={{0,7},{1,6},{2,5},{3,4},{4,3},{5,2},{6,1},{7,0},{8,15},{9,14},{10,... | collective-permute-start | bytes 2752520 | tf_op jit(solution)/shard_map/ppermute | solution.py:17
  111.5 19.1 %collective-permute-start.13 = (f32[128,1792]{1,0:T(8,128)}, f32[128,1792]{1,0:T(8,128)}, u32[]{:S(2)}, u32[]{:S(2)}) collective-permute-start(f32[128,1792]{1,0:T(8,128)} %calc.21), channel_id=1, source_target_pairs={{0,4},{1,5},{2,6},{3,7},{4,0},{5,1},{6,2},{7,3},{8,12},{9,13},{10,... | collective-permute-start | bytes 2752520 | tf_op jit(solution)/shard_map/ppermute | solution.py:17
  111.5 20.2 %collective-permute-start.14 = (f32[128,1792]{1,0:T(8,128)}, f32[128,1792]{1,0:T(8,128)}, u32[]{:S(2)}, u32[]{:S(2)}) collective-permute-start(f32[128,1792]{1,0:T(8,128)} %calc.22), channel_id=1, source_target_pairs={{0,2},{1,3},{2,0},{3,1},{4,6},{5,7},{6,4},{7,5},{8,10},{9,11},{10,... | collective-permute-start | bytes 2752520 | tf_op jit(solution)/shard_map/ppermute | solution.py:17
  117.0 19.4 %collective-permute-start.27 = (f32[256,1792]{1,0:T(8,128)}, f32[256,1792]{1,0:T(8,128)}, u32[]{:S(2)}, u32[]{:S(2)}) collective-permute-start(f32[256,1792]{1,0:T(8,128)} %cut.17), channel_id=1, source_target_pairs={{0,1},{1,0},{2,3},{3,2},{4,5},{5,4},{6,7},{7,6},{8,9},{9,8},{10,11... | collective-permute-start | bytes 5505032 | tf_op jit(solution)/shard_map/ppermute | solution.py:17
  125.7 44.1 %collective-permute-start.19 = (f32[256,1792]{1,0:T(8,128)}, f32[256,1792]{1,0:T(8,128)}, u32[]{:S(2)}, u32[]{:S(2)}) collective-permute-start(f32[256,1792]{1,0:T(8,128)} %cut.13), channel_id=1, source_target_pairs={{0,6},{1,7},{2,4},{3,5},{4,2},{5,3},{6,0},{7,1},{8,14},{9,15},{10,... | collective-permute-start | bytes 5505032 | tf_op jit(solution)/shard_map/ppermute | solution.py:17
  127.0 81.6 %collective-permute-start.17 = (f32[256,1792]{1,0:T(8,128)}, f32[256,1792]{1,0:T(8,128)}, u32[]{:S(2)}, u32[]{:S(2)}) collective-permute-start(f32[256,1792]{1,0:T(8,128)} %cut.12), channel_id=1, source_target_pairs={{0,5},{1,4},{2,7},{3,6},{4,1},{5,0},{6,3},{7,2},{8,13},{9,12},{10,... | collective-permute-start | bytes 5505032 | tf_op jit(solution)/shard_map/ppermute | solution.py:17
  130.6 82.9 %collective-permute-start.15 = (f32[256,1792]{1,0:T(8,128)}, f32[256,1792]{1,0:T(8,128)}, u32[]{:S(2)}, u32[]{:S(2)}) collective-permute-start(f32[256,1792]{1,0:T(8,128)} %cut.11), channel_id=1, source_target_pairs={{0,3},{1,2},{2,1},{3,0},{4,7},{5,6},{6,5},{7,4},{8,11},{9,10},{10,... | collective-permute-start | bytes 5505032 | tf_op jit(solution)/shard_map/ppermute | solution.py:17
  131.7 116.7 %collective-permute-start = (f32[256,1792]{1,0:T(8,128)}, f32[256,1792]{1,0:T(8,128)}, u32[]{:S(2)}, u32[]{:S(2)}) collective-permute-start(f32[256,1792]{1,0:T(8,128)} %cut.9), channel_id=1, source_target_pairs={{0,4},{1,5},{2,6},{3,7},{4,0},{5,1},{6,2},{7,3},{8,12},{9,13},{10,... | collective-permute-start | bytes 5505032 | tf_op jit(solution)/shard_map/ppermute | solution.py:17
  136.4 114.0 %collective-permute-start.7 = (f32[256,1792]{1,0:T(8,128)}, f32[256,1792]{1,0:T(8,128)}, u32[]{:S(2)}, u32[]{:S(2)}) collective-permute-start(f32[256,1792]{1,0:T(8,128)} %cut.10), channel_id=1, source_target_pairs={{0,2},{1,3},{2,0},{3,1},{4,6},{5,7},{6,4},{7,5},{8,10},{9,11},{10,... | collective-permute-start | bytes 5505032 | tf_op jit(solution)/shard_map/ppermute | solution.py:17
  169.8 85.8 %collective-permute-start.28 = (f32[256,1792]{1,0:T(8,128)}, f32[256,1792]{1,0:T(8,128)}, u32[]{:S(2)}, u32[]{:S(2)}) collective-permute-start(f32[256,1792]{1,0:T(8,128)} %calc.29), channel_id=1, source_target_pairs={{0,1},{1,0},{2,3},{3,2},{4,5},{5,4},{6,7},{7,6},{8,9},{9,8},{10,11... | collective-permute-start | bytes 5505032 | tf_op jit(solution)/shard_map/ppermute | solution.py:17
  208.6 79.2 %collective-permute-start.20 = (f32[256,1792]{1,0:T(8,128)}, f32[256,1792]{1,0:T(8,128)}, u32[]{:S(2)}, u32[]{:S(2)}) collective-permute-start(f32[256,1792]{1,0:T(8,128)} %calc.25), channel_id=1, source_target_pairs={{0,6},{1,7},{2,4},{3,5},{4,2},{5,3},{6,0},{7,1},{8,14},{9,15},{10,... | collective-permute-start | bytes 5505032 | tf_op jit(solution)/shard_map/ppermute | solution.py:17
  213.4 113.2 %collective-permute-start.18 = (f32[256,1792]{1,0:T(8,128)}, f32[256,1792]{1,0:T(8,128)}, u32[]{:S(2)}, u32[]{:S(2)}) collective-permute-start(f32[256,1792]{1,0:T(8,128)} %calc.24), channel_id=1, source_target_pairs={{0,5},{1,4},{2,7},{3,6},{4,1},{5,0},{6,3},{7,2},{8,13},{9,12},{10,... | collective-permute-start | bytes 5505032 | tf_op jit(solution)/shard_map/ppermute | solution.py:17
  248.4 78.4 %collective-permute-start.16 = (f32[256,1792]{1,0:T(8,128)}, f32[256,1792]{1,0:T(8,128)}, u32[]{:S(2)}, u32[]{:S(2)}) collective-permute-start(f32[256,1792]{1,0:T(8,128)} %calc.23), channel_id=1, source_target_pairs={{0,3},{1,2},{2,1},{3,0},{4,7},{5,6},{6,5},{7,4},{8,11},{9,10},{10,... | collective-permute-start | bytes 5505032 | tf_op jit(solution)/shard_map/ppermute | solution.py:17
  250.5 112.3 %collective-permute-start.12 = (f32[64,1792]{1,0:T(8,128)}, f32[64,1792]{1,0:T(8,128)}, u32[]{:S(2)}, u32[]{:S(2)}) collective-permute-start(f32[64,1792]{1,0:T(8,128)} %calc.20), channel_id=1, source_target_pairs={{0,2},{1,3},{2,0},{3,1},{4,6},{5,7},{6,4},{7,5},{8,10},{9,11},{10,... | collective-permute-start | bytes 1376264 | tf_op jit(solution)/shard_map/ppermute | solution.py:17
  255.6 110.7 %collective-permute-start.10 = (f32[32,1792]{1,0:T(8,128)}, f32[32,1792]{1,0:T(8,128)}, u32[]{:S(2)}, u32[]{:S(2)}) collective-permute-start(f32[32,1792]{1,0:T(8,128)} %calc.18), channel_id=1, source_target_pairs={{0,2},{1,3},{2,0},{3,1},{4,6},{5,7},{6,4},{7,5},{8,10},{9,11},{10,... | collective-permute-start | bytes 688136 | tf_op jit(solution)/shard_map/ppermute | solution.py:17
  287.8 78.4 %collective-permute-start.9 = (f32[32,1792]{1,0:T(8,128)}, f32[32,1792]{1,0:T(8,128)}, u32[]{:S(2)}, u32[]{:S(2)}) collective-permute-start(f32[32,1792]{1,0:T(8,128)} %calc.17), channel_id=1, source_target_pairs={{0,4},{1,5},{2,6},{3,7},{4,0},{5,1},{6,2},{7,3},{8,12},{9,13},{10,... | collective-permute-start | bytes 688136 | tf_op jit(solution)/shard_map/ppermute | solution.py:17
  326.6 42.6 %collective-permute-start.6 = (f32[32,1792]{1,0:T(8,128)}, f32[32,1792]{1,0:T(8,128)}, u32[]{:S(2)}, u32[]{:S(2)}) collective-permute-start(f32[32,1792]{1,0:T(8,128)} %calc.15), channel_id=1, source_target_pairs={{0,4},{1,5},{2,6},{3,7},{4,0},{5,1},{6,2},{7,3},{8,12},{9,13},{10,... | collective-permute-start | bytes 688136 | tf_op jit(solution)/shard_map/ppermute | solution.py:17
  326.8 42.3 %collective-permute-start.8 = (f32[32,1792]{1,0:T(8,128)}, f32[32,1792]{1,0:T(8,128)}, u32[]{:S(2)}, u32[]{:S(2)}) collective-permute-start(f32[32,1792]{1,0:T(8,128)} %calc.16), channel_id=1, source_target_pairs={{0,2},{1,3},{2,0},{3,1},{4,6},{5,7},{6,4},{7,5},{8,10},{9,11},{10,... | collective-permute-start | bytes 688136 | tf_op jit(solution)/shard_map/ppermute | solution.py:17
  (5 other events, 17.3 us)
where the time goes:
time: 373 us; the launch traced here: 372 us
  waiting for transfers between devices  227 us (61%)
  Pallas kernels  112 us (30%)
  starting transfers between devices  29.6 us (8%)
    ppermute x29, waiting for transfers between devices, hop(): return lax.ppermute(x, axis, [(i, i ^ k) for i in range(n)])  227 us
    pallas_call x11, Pallas kernels, finish(): pl.pallas_call(functools.partial(finish_kernel, parts), grid_spec=pltpu.P...  38.4 us
    pallas_call x15, Pallas kernels, calc(): pl.pallas_call(calc_kernel, grid_spec=pltpu.PrefetchScalarGridSpec(num_sc...  37.4 us
    ppermute x29, starting transfers between devices, hop(): return lax.ppermute(x, axis, [(i, i ^ k) for i in range(n)])  29.6 us
    pallas_call x9, Pallas kernels, cut(): pl.pallas_call(copy_kernel, grid_spec=pltpu.PrefetchScalarGridSpec(num_sc...  23.8 us
    pallas_call x1, Pallas kernels, squares(): pl.pallas_call(squares_kernel, grid=(rows // b,), in_specs=[pl.BlockSpec(...  8.04 us
  transfers between devices with their start and end apart: 29, of which 11 were waited for; matrix products, arithmetic and copies ran while one was open for 1% of the time, Pallas kernels for 29%

commit v1 on v0

--- a/solution.py
+++ b/solution.py
@@ -49,21 +49,22 @@
     )(at, x)
 
 
-def calc_kernel(at, factor, m_ref, g_ref, o_ref):
-    o_ref[...] = F32(0.9) * m_ref[...] + factor[0] * g_ref[...]
-
-
-def calc(m, g, factor, at, cols, start, rows):
-    b = block_rows(rows, start)
-    s = start // b
-    spec = pl.BlockSpec((b, cols), lambda i, at: (s + i, at[0]))
-    return pl.pallas_call(
-        calc_kernel,
-        grid_spec=pltpu.PrefetchScalarGridSpec(
-            num_scalar_prefetch=1, grid=(rows // b,),
+def calc_kernel(parcels, at, factor, m_ref, g_ref, *o_refs):
+    for (start, rows), o_ref in zip(parcels, o_refs):
+        part = pl.ds(start, rows)
+        o_ref[...] = F32(0.9) * m_ref[part, :] + factor[0] * g_ref[part, :]
+
+
+def calc(m, g, factor, at, cols, parcels):
+    rows = m.shape[0]
+    spec = pl.BlockSpec((rows, cols), lambda i, at: (0, at[0]))
+    return pl.pallas_call(
+        functools.partial(calc_kernel, parcels),
+        grid_spec=pltpu.PrefetchScalarGridSpec(
+            num_scalar_prefetch=1, grid=(1,),
             in_specs=[pl.BlockSpec(memory_space=pltpu.SMEM), spec, spec],
-            out_specs=pl.BlockSpec((b, cols), lambda i, at: (i, 0))),
-        out_shape=jax.ShapeDtypeStruct((rows, cols), F32),
+            out_specs=[pl.BlockSpec((r, cols), lambda i, at: (0, 0)) for _, r in parcels]),
+        out_shape=[jax.ShapeDtypeStruct((r, cols), F32) for _, r in parcels],
         cost_estimate=cost(3, rows, cols), name="calc", compiler_params=PARAMS,
     )(at, factor, m, g)
 
@@ -168,7 +169,7 @@
 def w_parcels(k, n, rows):
     e = rows // 8
     if e % 8 == 0 and k == n - 1:
-        return [(0, e), (e, 3 * e), (4 * e, 4 * e)]
+        return [(0, 2 * e), (2 * e, 2 * e), (4 * e, 4 * e)]
     return [(0, rows)]
 
 
@@ -209,8 +210,9 @@
     total = jnp.sum(part)
     factor = jnp.reshape(jnp.minimum(F32(1.0), limit / (jnp.sqrt(total) + F32(1e-06))), (1,))
     for k in far + near:
-        for j, (s, r) in enumerate(m_parcels(k, n, rows)):
-            moved_m[k, j] = hop(calc(momentum, grad, factor, at[k], cols, s, r), "col", k, n)
+        parts = calc(momentum, grad, factor, at[k], cols, m_parcels(k, n, rows))
+        for j, part in enumerate(parts):
+            moved_m[k, j] = hop(part, "col", k, n)
     outs = own(at[0], factor, weight, momentum, grad, n)
     for group in finish_order(n, rows):
         (s, r) = m_parcels(group[0][0], n, rows)[group[0][1]]

time: 373 us -> 395 us (1.059)
  waiting for transfers between devices: 227 us -> 260 us
  Pallas kernels: 112 us -> 97.3 us
    ppermute x29, waiting for transfers between devices: 227 us -> 260 us  [hop(): return lax.ppermute(x, axis, [(i, i ^ k) for i in range(n)])]
    pallas_call x15 -> x7, Pallas kernels: 37.4 us -> 24.1 us  [calc(): pl.pallas_call(functools.partial(calc_kernel, parcels), grid_spec=pltpu.P...]
  transfers between devices with their start and end apart: 29 -> 29, of which waited for: 11 -> 13; matrix products, arithmetic and copies ran while one was open for 1% -> 1% of each run, Pallas kernels for 29% -> 22%
where the time goes in v1:
time: 395 us; the launch traced here: 394 us
  waiting for transfers between devices  260 us (66%)
  Pallas kernels  97.3 us (25%)
  starting transfers between devices  32 us (8%)
    ppermute x29, waiting for transfers between devices, hop(): return lax.ppermute(x, axis, [(i, i ^ k) for i in range(n)])  260 us
    pallas_call x11, Pallas kernels, finish(): pl.pallas_call(functools.partial(finish_kernel, parts), grid_spec=pltpu.P...  37.5 us
    ppermute x29, starting transfers between devices, hop(): return lax.ppermute(x, axis, [(i, i ^ k) for i in range(n)])  32 us
    pallas_call x7, Pallas kernels, calc(): pl.pallas_call(functools.partial(calc_kernel, parcels), grid_spec=pltpu.P...  24.1 us
    pallas_call x9, Pallas kernels, cut(): pl.pallas_call(copy_kernel, grid_spec=pltpu.PrefetchScalarGridSpec(num_sc...  23 us
    pallas_call x1, Pallas kernels, squares(): pl.pallas_call(squares_kernel, grid=(rows // b,), in_specs=[pl.BlockSpec(...  8.05 us
  transfers between devices with their start and end apart: 29, of which 13 were waited for; matrix products, arithmetic and copies ran while one was open for 1% of the time, Pallas kernels for 22%

profile of v1, /device:TPU:0, one launch (start us, length us, event | category | flops | bytes accessed | tf_op | source)
XLA Modules:
  0.0 393.8 jit_solution(1073286462360339255)
XLA Ops:
  0.6 8.1 %squares.1 = f32[8,128]{1,0:T(8,128)} custom-call(f32[256,14336]{1,0:T(8,128)} %g_ref.17), custom_call_target="tpu_custom_call" | custom-call | flops 14680064 | bytes 14680064 | tf_op jit(solution)/shard_map/squares/pallas_call | solution.py:154
  34.4 3.4 calc.12
  42.6 3.3 calc.7
  48.6 3.1 collective-permute-done.23.refs_0_
  53.2 3.3 calc.8
  56.6 5.1 %collective-permute-done.26.refs_1_ = f32[64,1792]{1,0:T(8,128)} collective-permute-done((f32[64,1792]{1,0:T(8,128)}, f32[64,1792]{1,0:T(8,128)}, u32[]{:S(2)}, u32[]{:S(2)}) %collective-permute-start.26) | collective-permute-done | bytes 458784 | tf_op jit(solution)/shard_map/ppermute | solution.py:17
  61.7 9.8 %collective-permute-done.24.refs_1_ = f32[64,1792]{1,0:T(8,128)} collective-permute-done((f32[64,1792]{1,0:T(8,128)}, f32[64,1792]{1,0:T(8,128)}, u32[]{:S(2)}, u32[]{:S(2)}) %collective-permute-start.24) | collective-permute-done | bytes 458784 | tf_op jit(solution)/shard_map/ppermute | solution.py:17
  75.8 63.5 %collective-permute-done.11.refs_1_ = f32[64,1792]{1,0:T(8,128)} collective-permute-done((f32[64,1792]{1,0:T(8,128)}, f32[64,1792]{1,0:T(8,128)}, u32[]{:S(2)}, u32[]{:S(2)}) %collective-permute-start.11) | collective-permute-done | bytes 458784 | tf_op jit(solution)/shard_map/ppermute | solution.py:17
  159.0 3.5 calc.13
  162.5 3.5 calc.11
  166.0 3.5 calc.10
  169.5 22.7 %collective-permute-done.19.refs_0_ = f32[256,1792]{1,0:T(8,128)} collective-permute-done((f32[256,1792]{1,0:T(8,128)}, f32[256,1792]{1,0:T(8,128)}, u32[]{:S(2)}, u32[]{:S(2)}) %collective-permute-start.19) | collective-permute-done | bytes 1835040 | tf_op jit(solution)/shard_map/ppermute | solution.py:17
  192.2 38.8 %collective-permute-done.17.refs_0_ = f32[256,1792]{1,0:T(8,128)} collective-permute-done((f32[256,1792]{1,0:T(8,128)}, f32[256,1792]{1,0:T(8,128)}, u32[]{:S(2)}, u32[]{:S(2)}) %collective-permute-start.17) | collective-permute-done | bytes 1835040 | tf_op jit(solution)/shard_map/ppermute | solution.py:17
  232.6 3.6 calc.9
  236.2 34.6 %collective-permute-done.refs_0_ = f32[256,1792]{1,0:T(8,128)} collective-permute-done((f32[256,1792]{1,0:T(8,128)}, f32[256,1792]{1,0:T(8,128)}, u32[]{:S(2)}, u32[]{:S(2)}) %collective-permute-start) | collective-permute-done | bytes 1835040 | tf_op jit(solution)/shard_map/ppermute | solution.py:17
  272.8 37.4 %collective-permute-done.20.refs_1_ = f32[256,1792]{1,0:T(8,128)} collective-permute-done((f32[256,1792]{1,0:T(8,128)}, f32[256,1792]{1,0:T(8,128)}, u32[]{:S(2)}, u32[]{:S(2)}) %collective-permute-start.20) | collective-permute-done | bytes 1835040 | tf_op jit(solution)/shard_map/ppermute | solution.py:17
  310.4 38.6 %collective-permute-done.18.refs_1_ = f32[256,1792]{1,0:T(8,128)} collective-permute-done((f32[256,1792]{1,0:T(8,128)}, f32[256,1792]{1,0:T(8,128)}, u32[]{:S(2)}, u32[]{:S(2)}) %collective-permute-start.18) | collective-permute-done | bytes 1835040 | tf_op jit(solution)/shard_map/ppermute | solution.py:17
  351.6 4.7 %own.1 = (f32[2048,1792]{1,0:T(8,128)}, f32[2048,1792]{1,0:T(8,128)}) custom-call(s32[1]{0:T(128)} %bitcast.8.at, f32[1]{0:T(128)} %bitcast.2.factor, f32[256,14336]{1,0:T(8,128)} %w_ref.1, f32[256,14336]{1,0:T(8,128)} %m_ref.15, f32[256,14336]{1,0:T(8,128)} %g_ref.17), custom_call_target="tpu_custom_call" | custom-call | flops 1835008 | bytes 9175040 | tf_op jit(solution)/shard_map/own/pallas_call | solution.py:121
  356.2 4.1 %finish.11 = (f32[2048,1792]{1,0:T(8,128)}, f32[2048,1792]{1,0:T(8,128)}) custom-call(s32[1]{0:T(128)} %bitcast.7.at, f32[256,1792]{1,0:T(8,128)} %collective-permute-done.27.refs_0_, f32[256,1792]{1,0:T(8,128)} %collective-permute-done.28.refs_1_, f32[2048,1792]{1,0:T(8,128)} %get-tuple-element.46.refs_2_, ...), custom_call_target="tpu_custom_call", output_to_operand_aliasing={{0}: (3, {}), {1}: (4, {})} | custom-call | flops 1835008 | bytes 7340032 | tf_op jit(solution)/shard_map/finish/pallas_call | solution.py:98
  367.4 4.1 %finish.15 = (f32[2048,1792]{1,0:T(8,128)}, f32[2048,1792]{1,0:T(8,128)}) custom-call(s32[1]{0:T(128)} %bitcast.5.at, f32[256,1792]{1,0:T(8,128)} %collective-permute-done.19.refs_0_, f32[256,1792]{1,0:T(8,128)} %collective-permute-done.20.refs_1_, f32[2048,1792]{1,0:T(8,128)} %get-tuple-element.54.refs_2_, ...), custom_call_target="tpu_custom_call", output_to_operand_aliasing={{0}: (3, {}), {1}: (4, {})} | custom-call | flops 1835008 | bytes 7340032 | tf_op jit(solution)/shard_map/finish/pallas_call | solution.py:98
  371.5 4.1 %finish.16 = (f32[2048,1792]{1,0:T(8,128)}, f32[2048,1792]{1,0:T(8,128)}) custom-call(s32[1]{0:T(128)} %bitcast.4.at, f32[256,1792]{1,0:T(8,128)} %collective-permute-done.17.refs_0_, f32[256,1792]{1,0:T(8,128)} %collective-permute-done.18.refs_1_, f32[2048,1792]{1,0:T(8,128)} %get-tuple-element.56.refs_2_, ...), custom_call_target="tpu_custom_call", output_to_operand_aliasing={{0}: (3, {}), {1}: (4, {})} | custom-call | flops 1835008 | bytes 7340032 | tf_op jit(solution)/shard_map/finish/pallas_call | solution.py:98
  375.6 4.1 %finish.17 = (f32[2048,1792]{1,0:T(8,128)}, f32[2048,1792]{1,0:T(8,128)}) custom-call(s32[1]{0:T(128)} %bitcast.3.at, f32[256,1792]{1,0:T(8,128)} %collective-permute-done.15.refs_0_, f32[256,1792]{1,0:T(8,128)} %collective-permute-done.16.refs_1_, f32[2048,1792]{1,0:T(8,128)} %get-tuple-element.58.refs_2_, ...), custom_call_target="tpu_custom_call", output_to_operand_aliasing={{0}: (3, {}), {1}: (4, {})} | custom-call | flops 1835008 | bytes 7340032 | tf_op jit(solution)/shard_map/finish/pallas_call | solution.py:98
  379.7 4.7 %finish.18 = (f32[2048,1792]{1,0:T(8,128)}, f32[2048,1792]{1,0:T(8,128)}) custom-call(s32[2]{0:T(128)} %pad_add_fusion.at, f32[256,1792]{1,0:T(8,128)} %collective-permute-done.refs_0_, f32[128,1792]{1,0:T(8,128)} %collective-permute-done.13.refs_1_, f32[256,1792]{1,0:T(8,128)} %collective-permute-done.7.refs_2_, ...), custom_call_target="tpu_custom_call", output_to_operand_aliasing={{0}: (5, {}), {1}: (6, {})} | custom-call | flops 917504 | bytes 7340032 | tf_op jit(solution)/shard_map/finish/pallas_call | solution.py:98
  384.4 3.4 finish.19
  (69 shorter events, 77.4 us)
Async XLA Ops:
  27.9 18.1 %collective-permute-start.25 = (f32[64,1792]{1,0:T(8,128)}, f32[64,1792]{1,0:T(8,128)}, u32[]{:S(2)}, u32[]{:S(2)}) collective-permute-start(f32[64,1792]{1,0:T(8,128)} %cut.16), channel_id=1, source_target_pairs={{0,7},{1,6},{2,5},{3,4},{4,3},{5,2},{6,1},{7,0},{8,15},{9,14},{10,... | collective-permute-start | bytes 1376264 | tf_op jit(solution)/shard_map/ppermute | solution.py:17
  29.7 22.0 %collective-permute-start.23 = (f32[64,1792]{1,0:T(8,128)}, f32[64,1792]{1,0:T(8,128)}, u32[]{:S(2)}, u32[]{:S(2)}) collective-permute-start(f32[64,1792]{1,0:T(8,128)} %cut.15), channel_id=1, source_target_pairs={{0,7},{1,6},{2,5},{3,4},{4,3},{5,2},{6,1},{7,0},{8,15},{9,14},{10,... | collective-permute-start | bytes 1376264 | tf_op jit(solution)/shard_map/ppermute | solution.py:17
  37.8 23.9 %collective-permute-start.26 = (f32[64,1792]{1,0:T(8,128)}, f32[64,1792]{1,0:T(8,128)}, u32[]{:S(2)}, u32[]{:S(2)}) collective-permute-start(f32[64,1792]{1,0:T(8,128)} %get-tuple-element.45), channel_id=1, source_target_pairs={{0,7},{1,6},{2,5},{3,4},{4,3},{5,2},{6,1},{7,0},{8,15},{9,14},{10,... | collective-permute-start | bytes 1376264 | tf_op jit(solution)/shard_map/ppermute | solution.py:17
  37.8 33.7 %collective-permute-start.24 = (f32[64,1792]{1,0:T(8,128)}, f32[64,1792]{1,0:T(8,128)}, u32[]{:S(2)}, u32[]{:S(2)}) collective-permute-start(f32[64,1792]{1,0:T(8,128)} %get-tuple-element.44), channel_id=1, source_target_pairs={{0,7},{1,6},{2,5},{3,4},{4,3},{5,2},{6,1},{7,0},{8,15},{9,14},{10,... | collective-permute-start | bytes 1376264 | tf_op jit(solution)/shard_map/ppermute | solution.py:17
  42.6 105.4 %collective-permute-start.21 = (f32[128,1792]{1,0:T(8,128)}, f32[128,1792]{1,0:T(8,128)}, u32[]{:S(2)}, u32[]{:S(2)}) collective-permute-start(f32[128,1792]{1,0:T(8,128)} %cut.14), channel_id=1, source_target_pairs={{0,7},{1,6},{2,5},{3,4},{4,3},{5,2},{6,1},{7,0},{8,15},{9,14},{10,... | collective-permute-start | bytes 2752520 | tf_op jit(solution)/shard_map/ppermute | solution.py:17
  46.0 103.5 %collective-permute-start.22 = (f32[128,1792]{1,0:T(8,128)}, f32[128,1792]{1,0:T(8,128)}, u32[]{:S(2)}, u32[]{:S(2)}) collective-permute-start(f32[128,1792]{1,0:T(8,128)} %get-tuple-element.43), channel_id=1, source_target_pairs={{0,7},{1,6},{2,5},{3,4},{4,3},{5,2},{6,1},{7,0},{8,15},{9,14},{10,... | collective-permute-start | bytes 2752520 | tf_op jit(solution)/shard_map/ppermute | solution.py:17
  51.7 98.7 %collective-permute-start.13 = (f32[128,1792]{1,0:T(8,128)}, f32[128,1792]{1,0:T(8,128)}, u32[]{:S(2)}, u32[]{:S(2)}) collective-permute-start(f32[128,1792]{1,0:T(8,128)} %get-tuple-element.41), channel_id=1, source_target_pairs={{0,4},{1,5},{2,6},{3,7},{4,0},{5,1},{6,2},{7,3},{8,12},{9,13},{10,... | collective-permute-start | bytes 2752520 | tf_op jit(solution)/shard_map/ppermute | solution.py:17
  61.7 92.4 %collective-permute-start.14 = (f32[128,1792]{1,0:T(8,128)}, f32[128,1792]{1,0:T(8,128)}, u32[]{:S(2)}, u32[]{:S(2)}) collective-permute-start(f32[128,1792]{1,0:T(8,128)} %get-tuple-element.42), channel_id=1, source_target_pairs={{0,2},{1,3},{2,0},{3,1},{4,6},{5,7},{6,4},{7,5},{8,10},{9,11},{10,... | collective-permute-start | bytes 2752520 | tf_op jit(solution)/shard_map/ppermute | solution.py:17
  71.5 67.9 %collective-permute-start.11 = (f32[64,1792]{1,0:T(8,128)}, f32[64,1792]{1,0:T(8,128)}, u32[]{:S(2)}, u32[]{:S(2)}) collective-permute-start(f32[64,1792]{1,0:T(8,128)} %get-tuple-element.39), channel_id=1, source_target_pairs={{0,4},{1,5},{2,6},{3,7},{4,0},{5,1},{6,2},{7,3},{8,12},{9,13},{10,... | collective-permute-start | bytes 1376264 | tf_op jit(solution)/shard_map/ppermute | solution.py:17
  139.3 17.8 %collective-permute-start.27 = (f32[256,1792]{1,0:T(8,128)}, f32[256,1792]{1,0:T(8,128)}, u32[]{:S(2)}, u32[]{:S(2)}) collective-permute-start(f32[256,1792]{1,0:T(8,128)} %cut.17), channel_id=1, source_target_pairs={{0,1},{1,0},{2,3},{3,2},{4,5},{5,4},{6,7},{7,6},{8,9},{9,8},{10,11... | collective-permute-start | bytes 5505032 | tf_op jit(solution)/shard_map/ppermute | solution.py:17
  148.0 44.1 %collective-permute-start.19 = (f32[256,1792]{1,0:T(8,128)}, f32[256,1792]{1,0:T(8,128)}, u32[]{:S(2)}, u32[]{:S(2)}) collective-permute-start(f32[256,1792]{1,0:T(8,128)} %cut.13), channel_id=1, source_target_pairs={{0,6},{1,7},{2,4},{3,5},{4,2},{5,3},{6,0},{7,1},{8,14},{9,15},{10,... | collective-permute-start | bytes 5505032 | tf_op jit(solution)/shard_map/ppermute | solution.py:17
  149.5 81.5 %collective-permute-start.17 = (f32[256,1792]{1,0:T(8,128)}, f32[256,1792]{1,0:T(8,128)}, u32[]{:S(2)}, u32[]{:S(2)}) collective-permute-start(f32[256,1792]{1,0:T(8,128)} %cut.12), channel_id=1, source_target_pairs={{0,5},{1,4},{2,7},{3,6},{4,1},{5,0},{6,3},{7,2},{8,13},{9,12},{10,... | collective-permute-start | bytes 5505032 | tf_op jit(solution)/shard_map/ppermute | solution.py:17
  150.4 82.0 %collective-permute-start.15 = (f32[256,1792]{1,0:T(8,128)}, f32[256,1792]{1,0:T(8,128)}, u32[]{:S(2)}, u32[]{:S(2)}) collective-permute-start(f32[256,1792]{1,0:T(8,128)} %cut.11), channel_id=1, source_target_pairs={{0,3},{1,2},{2,1},{3,0},{4,7},{5,6},{6,5},{7,4},{8,11},{9,10},{10,... | collective-permute-start | bytes 5505032 | tf_op jit(solution)/shard_map/ppermute | solution.py:17
  154.1 116.7 %collective-permute-start = (f32[256,1792]{1,0:T(8,128)}, f32[256,1792]{1,0:T(8,128)}, u32[]{:S(2)}, u32[]{:S(2)}) collective-permute-start(f32[256,1792]{1,0:T(8,128)} %cut.9), channel_id=1, source_target_pairs={{0,4},{1,5},{2,6},{3,7},{4,0},{5,1},{6,2},{7,3},{8,12},{9,13},{10,... | collective-permute-start | bytes 5505032 | tf_op jit(solution)/shard_map/ppermute | solution.py:17
  157.1 113.7 %collective-permute-start.7 = (f32[256,1792]{1,0:T(8,128)}, f32[256,1792]{1,0:T(8,128)}, u32[]{:S(2)}, u32[]{:S(2)}) collective-permute-start(f32[256,1792]{1,0:T(8,128)} %cut.10), channel_id=1, source_target_pairs={{0,2},{1,3},{2,0},{3,1},{4,6},{5,7},{6,4},{7,5},{8,10},{9,11},{10,... | collective-permute-start | bytes 5505032 | tf_op jit(solution)/shard_map/ppermute | solution.py:17
  192.2 80.2 %collective-permute-start.28 = (f32[256,1792]{1,0:T(8,128)}, f32[256,1792]{1,0:T(8,128)}, u32[]{:S(2)}, u32[]{:S(2)}) collective-permute-start(f32[256,1792]{1,0:T(8,128)} %calc.13), channel_id=1, source_target_pairs={{0,1},{1,0},{2,3},{3,2},{4,5},{5,4},{6,7},{7,6},{8,9},{9,8},{10,11... | collective-permute-start | bytes 5505032 | tf_op jit(solution)/shard_map/ppermute | solution.py:17
  231.0 79.2 %collective-permute-start.20 = (f32[256,1792]{1,0:T(8,128)}, f32[256,1792]{1,0:T(8,128)}, u32[]{:S(2)}, u32[]{:S(2)}) collective-permute-start(f32[256,1792]{1,0:T(8,128)} %calc.11), channel_id=1, source_target_pairs={{0,6},{1,7},{2,4},{3,5},{4,2},{5,3},{6,0},{7,1},{8,14},{9,15},{10,... | collective-permute-start | bytes 5505032 | tf_op jit(solution)/shard_map/ppermute | solution.py:17
  232.4 116.5 %collective-permute-start.18 = (f32[256,1792]{1,0:T(8,128)}, f32[256,1792]{1,0:T(8,128)}, u32[]{:S(2)}, u32[]{:S(2)}) collective-permute-start(f32[256,1792]{1,0:T(8,128)} %calc.10), channel_id=1, source_target_pairs={{0,5},{1,4},{2,7},{3,6},{4,1},{5,0},{6,3},{7,2},{8,13},{9,12},{10,... | collective-permute-start | bytes 5505032 | tf_op jit(solution)/shard_map/ppermute | solution.py:17
  270.8 78.3 %collective-permute-start.16 = (f32[256,1792]{1,0:T(8,128)}, f32[256,1792]{1,0:T(8,128)}, u32[]{:S(2)}, u32[]{:S(2)}) collective-permute-start(f32[256,1792]{1,0:T(8,128)} %calc.9), channel_id=1, source_target_pairs={{0,3},{1,2},{2,1},{3,0},{4,7},{5,6},{6,5},{7,4},{8,11},{9,10},{10,... | collective-permute-start | bytes 5505032 | tf_op jit(solution)/shard_map/ppermute | solution.py:17
  270.8 113.6 %collective-permute-start.12 = (f32[64,1792]{1,0:T(8,128)}, f32[64,1792]{1,0:T(8,128)}, u32[]{:S(2)}, u32[]{:S(2)}) collective-permute-start(f32[64,1792]{1,0:T(8,128)} %get-tuple-element.40), channel_id=1, source_target_pairs={{0,2},{1,3},{2,0},{3,1},{4,6},{5,7},{6,4},{7,5},{8,10},{9,11},{10,... | collective-permute-start | bytes 1376264 | tf_op jit(solution)/shard_map/ppermute | solution.py:17
  272.4 115.5 %collective-permute-start.10 = (f32[32,1792]{1,0:T(8,128)}, f32[32,1792]{1,0:T(8,128)}, u32[]{:S(2)}, u32[]{:S(2)}) collective-permute-start(f32[32,1792]{1,0:T(8,128)} %get-tuple-element.38), channel_id=1, source_target_pairs={{0,2},{1,3},{2,0},{3,1},{4,6},{5,7},{6,4},{7,5},{8,10},{9,11},{10,... | collective-permute-start | bytes 688136 | tf_op jit(solution)/shard_map/ppermute | solution.py:17
  310.2 77.7 %collective-permute-start.9 = (f32[32,1792]{1,0:T(8,128)}, f32[32,1792]{1,0:T(8,128)}, u32[]{:S(2)}, u32[]{:S(2)}) collective-permute-start(f32[32,1792]{1,0:T(8,128)} %get-tuple-element.37), channel_id=1, source_target_pairs={{0,4},{1,5},{2,6},{3,7},{4,0},{5,1},{6,2},{7,3},{8,12},{9,13},{10,... | collective-permute-start | bytes 688136 | tf_op jit(solution)/shard_map/ppermute | solution.py:17
  348.9 41.9 %collective-permute-start.6 = (f32[32,1792]{1,0:T(8,128)}, f32[32,1792]{1,0:T(8,128)}, u32[]{:S(2)}, u32[]{:S(2)}) collective-permute-start(f32[32,1792]{1,0:T(8,128)} %get-tuple-element.35), channel_id=1, source_target_pairs={{0,4},{1,5},{2,6},{3,7},{4,0},{5,1},{6,2},{7,3},{8,12},{9,13},{10,... | collective-permute-start | bytes 688136 | tf_op jit(solution)/shard_map/ppermute | solution.py:17
  349.1 41.7 %collective-permute-start.8 = (f32[32,1792]{1,0:T(8,128)}, f32[32,1792]{1,0:T(8,128)}, u32[]{:S(2)}, u32[]{:S(2)}) collective-permute-start(f32[32,1792]{1,0:T(8,128)} %get-tuple-element.36), channel_id=1, source_target_pairs={{0,2},{1,3},{2,0},{3,1},{4,6},{5,7},{6,4},{7,5},{8,10},{9,11},{10,... | collective-permute-start | bytes 688136 | tf_op jit(solution)/shard_map/ppermute | solution.py:17
  (5 other events, 22.3 us)

commit v2 on v1

--- a/solution.py
+++ b/solution.py
@@ -106,6 +106,48 @@
     )(at, *[x for pair in pairs for x in pair], *outs)
 
 
+def last_finish_kernel(parts, s, p, rows, chunk, at, *refs):
+    ins, (nw_hbm, nm_hbm), scratch = refs[:2 * parts], refs[2 * parts + 2:2 * parts + 4], refs[2 * parts + 4:]
+    bufs, news, in_sem, out_sem = scratch[:2 * parts], scratch[2 * parts:3 * parts], scratch[-2], scratch[-1]
+    chunks = [(q, r) for r in range(0, rows, chunk) for q in range(parts)]
+
+    def load(q, j, r):
+        ref = ins[2 * q + j]
+        here = pl.ds(r, chunk)
+        return pltpu.make_async_copy(ref.at[pl.ds(ref.shape[0] - rows + r, chunk)], bufs[2 * q + j].at[here], in_sem.at[2 * q + j, r // chunk])
+
+    loads = {(q, j, r): load(q, j, r) for q, r in chunks for j in (1, 0)}
+    for copy in loads.values():
+        copy.start()
+    stores = []
+    for q, r in chunks:
+        out = pl.ds(pl.multiple_of((at[q] * p + s) * rows + r, 8), chunk)
+        here = pl.ds(r, chunk)
+        loads[q, 1, r].wait()
+        stores.append(pltpu.make_async_copy(bufs[2 * q + 1].at[here], nm_hbm.at[out], out_sem.at[2 * q + 1, r // chunk]))
+        stores[-1].start()
+        loads[q, 0, r].wait()
+        news[q][here] = bufs[2 * q][here] - F32(0.1) * bufs[2 * q + 1][here]
+        stores.append(pltpu.make_async_copy(news[q].at[here], nw_hbm.at[out], out_sem.at[2 * q, r // chunk]))
+        stores[-1].start()
+    for copy in stores:
+        copy.wait()
+
+
+def last_finish(at, pairs, outs, shape, piece, start, rows):
+    cols = shape[1]
+    parts = len(pairs)
+    hbm = pl.BlockSpec(memory_space=pl.ANY)
+    return pl.pallas_call(
+        functools.partial(last_finish_kernel, parts, start // rows, piece // rows, rows, rows),
+        in_specs=[pl.BlockSpec(memory_space=pltpu.SMEM)] + [hbm] * (2 * parts + 2), out_specs=[hbm, hbm],
+        out_shape=[jax.ShapeDtypeStruct(shape, F32)] * 2,
+        input_output_aliases={2 * parts + 1: 0, 2 * parts + 2: 1},
+        scratch_shapes=[pltpu.VMEM((rows, cols), F32)] * (3 * parts) + [pltpu.SemaphoreType.DMA((2 * parts, 1))] * 2,
+        cost_estimate=cost(4 * parts, rows, cols), name="last_finish", compiler_params=PARAMS,
+    )(at, *[x for pair in pairs for x in pair], *outs)
+
+
 def own_kernel(at, factor, w_ref, m_ref, g_ref, nw_ref, nm_ref):
     m = F32(0.9) * m_ref[...] + factor[0] * g_ref[...]
     nm_ref[...] = m
@@ -163,7 +205,7 @@
 
 
 def last_pair(n):
-    return [k for k in (4, 2) if k < n]
+    return [k for k in (2, 4) if k < n]
 
 
 def w_parcels(k, n, rows):
@@ -222,7 +264,10 @@
             pairs.append((moved_w[k, i], moved_m[k, j]))
             where.append(at[k])
         within = s - w_parcels(group[0][0], n, rows)[i][0]
-        outs = finish(jnp.concatenate(where), pairs, outs, (rows * n, cols), rows, s, r, within)
+        if s + r == rows and s and len(group) > 1:
+            outs = last_finish(jnp.concatenate(where), pairs, outs, (rows * n, cols), rows, s, r)
+        else:
+            outs = finish(jnp.concatenate(where), pairs, outs, (rows * n, cols), rows, s, r, within)
     return tuple(outs)
 
 

time: 395 us -> 393 us (level)
  waiting for transfers between devices: 260 us -> 255 us
    ppermute x29, waiting for transfers between devices: 260 us -> 255 us  [hop(): return lax.ppermute(x, axis, [(i, i ^ k) for i in range(n)])]
    pallas_call x11 -> x10, Pallas kernels: 37.5 us -> 34.6 us  [finish(): pl.pallas_call(functools.partial(finish_kernel, parts), grid_spec=pltpu.P...]
where the time goes in v2:
time: 393 us; the launch traced here: 392 us
  waiting for transfers between devices  255 us (65%)
  Pallas kernels  97.1 us (25%)
  starting transfers between devices  35.6 us (9%)
    ppermute x29, waiting for transfers between devices, hop(): return lax.ppermute(x, axis, [(i, i ^ k) for i in range(n)])  255 us
    ppermute x29, starting transfers between devices, hop(): return lax.ppermute(x, axis, [(i, i ^ k) for i in range(n)])  35.6 us
    pallas_call x10, Pallas kernels, finish(): pl.pallas_call(functools.partial(finish_kernel, parts), grid_spec=pltpu.P...  34.6 us
    pallas_call x7, Pallas kernels, calc(): pl.pallas_call(functools.partial(calc_kernel, parcels), grid_spec=pltpu.P...  24.1 us
    pallas_call x9, Pallas kernels, cut(): pl.pallas_call(copy_kernel, grid_spec=pltpu.PrefetchScalarGridSpec(num_sc...  23 us
    pallas_call x1, Pallas kernels, squares(): pl.pallas_call(squares_kernel, grid=(rows // b,), in_specs=[pl.BlockSpec(...  8.05 us
  transfers between devices with their start and end apart: 29, of which 13 were waited for; matrix products, arithmetic and copies ran while one was open for 1% of the time, Pallas kernels for 22%

profile of v2, /device:TPU:0, one launch (start us, length us, event | category | flops | bytes accessed | tf_op | source)
XLA Modules:
  0.0 392.3 jit_solution(16641969229839649066)
XLA Ops:
  0.6 8.1 %squares.1 = f32[8,128]{1,0:T(8,128)} custom-call(f32[256,14336]{1,0:T(8,128)} %g_ref.17), custom_call_target="tpu_custom_call" | custom-call | flops 14680064 | bytes 14680064 | tf_op jit(solution)/shard_map/squares/pallas_call | solution.py:196
  34.4 3.4 calc.12
  42.6 3.3 calc.7
  48.6 3.1 collective-permute-done.23.refs_0_
  51.7 3.3 calc.8
  55.0 6.5 %collective-permute-done.26.refs_1_ = f32[64,1792]{1,0:T(8,128)} collective-permute-done((f32[64,1792]{1,0:T(8,128)}, f32[64,1792]{1,0:T(8,128)}, u32[]{:S(2)}, u32[]{:S(2)}) %collective-permute-start.26) | collective-permute-done | bytes 458784 | tf_op jit(solution)/shard_map/ppermute | solution.py:17
  63.1 8.4 %collective-permute-done.24.refs_1_ = f32[64,1792]{1,0:T(8,128)} collective-permute-done((f32[64,1792]{1,0:T(8,128)}, f32[64,1792]{1,0:T(8,128)}, u32[]{:S(2)}, u32[]{:S(2)}) %collective-permute-start.24) | collective-permute-done | bytes 458784 | tf_op jit(solution)/shard_map/ppermute | solution.py:17
  74.3 62.2 %collective-permute-done.11.refs_1_ = f32[64,1792]{1,0:T(8,128)} collective-permute-done((f32[64,1792]{1,0:T(8,128)}, f32[64,1792]{1,0:T(8,128)}, u32[]{:S(2)}, u32[]{:S(2)}) %collective-permute-start.11) | collective-permute-done | bytes 458784 | tf_op jit(solution)/shard_map/ppermute | solution.py:17
  158.6 3.5 calc.13
  162.1 3.5 calc.11
  165.6 3.5 calc.10
  169.1 21.6 %collective-permute-done.19.refs_0_ = f32[256,1792]{1,0:T(8,128)} collective-permute-done((f32[256,1792]{1,0:T(8,128)}, f32[256,1792]{1,0:T(8,128)}, u32[]{:S(2)}, u32[]{:S(2)}) %collective-permute-start.19) | collective-permute-done | bytes 1835040 | tf_op jit(solution)/shard_map/ppermute | solution.py:17
  190.7 38.7 %collective-permute-done.17.refs_0_ = f32[256,1792]{1,0:T(8,128)} collective-permute-done((f32[256,1792]{1,0:T(8,128)}, f32[256,1792]{1,0:T(8,128)}, u32[]{:S(2)}, u32[]{:S(2)}) %collective-permute-start.17) | collective-permute-done | bytes 1835040 | tf_op jit(solution)/shard_map/ppermute | solution.py:17
  231.8 3.6 calc.9
  235.4 34.4 %collective-permute-done.refs_0_ = f32[256,1792]{1,0:T(8,128)} collective-permute-done((f32[256,1792]{1,0:T(8,128)}, f32[256,1792]{1,0:T(8,128)}, u32[]{:S(2)}, u32[]{:S(2)}) %collective-permute-start) | collective-permute-done | bytes 1835040 | tf_op jit(solution)/shard_map/ppermute | solution.py:17
  271.9 36.9 %collective-permute-done.20.refs_1_ = f32[256,1792]{1,0:T(8,128)} collective-permute-done((f32[256,1792]{1,0:T(8,128)}, f32[256,1792]{1,0:T(8,128)}, u32[]{:S(2)}, u32[]{:S(2)}) %collective-permute-start.20) | collective-permute-done | bytes 1835040 | tf_op jit(solution)/shard_map/ppermute | solution.py:17
  310.6 36.8 %collective-permute-done.18.refs_1_ = f32[256,1792]{1,0:T(8,128)} collective-permute-done((f32[256,1792]{1,0:T(8,128)}, f32[256,1792]{1,0:T(8,128)}, u32[]{:S(2)}, u32[]{:S(2)}) %collective-permute-start.18) | collective-permute-done | bytes 1835040 | tf_op jit(solution)/shard_map/ppermute | solution.py:17
  350.3 4.7 %own.1 = (f32[2048,1792]{1,0:T(8,128)}, f32[2048,1792]{1,0:T(8,128)}) custom-call(s32[1]{0:T(128)} %bitcast.8.at, f32[1]{0:T(128)} %bitcast.2.factor, f32[256,14336]{1,0:T(8,128)} %w_ref.1, f32[256,14336]{1,0:T(8,128)} %m_ref.15, f32[256,14336]{1,0:T(8,128)} %g_ref.17), custom_call_target="tpu_custom_call" | custom-call | flops 1835008 | bytes 9175040 | tf_op jit(solution)/shard_map/own/pallas_call | solution.py:163
  354.9 4.1 %finish.10 = (f32[2048,1792]{1,0:T(8,128)}, f32[2048,1792]{1,0:T(8,128)}) custom-call(s32[1]{0:T(128)} %bitcast.7.at, f32[256,1792]{1,0:T(8,128)} %collective-permute-done.27.refs_0_, f32[256,1792]{1,0:T(8,128)} %collective-permute-done.28.refs_1_, f32[2048,1792]{1,0:T(8,128)} %get-tuple-element.46.refs_2_, ...), custom_call_target="tpu_custom_call", output_to_operand_aliasing={{0}: (3, {}), {1}: (4, {})} | custom-call | flops 1835008 | bytes 7340032 | tf_op jit(solution)/shard_map/finish/pallas_call | solution.py:98
  366.1 4.1 %finish.14 = (f32[2048,1792]{1,0:T(8,128)}, f32[2048,1792]{1,0:T(8,128)}) custom-call(s32[1]{0:T(128)} %bitcast.5.at, f32[256,1792]{1,0:T(8,128)} %collective-permute-done.19.refs_0_, f32[256,1792]{1,0:T(8,128)} %collective-permute-done.20.refs_1_, f32[2048,1792]{1,0:T(8,128)} %get-tuple-element.54.refs_2_, ...), custom_call_target="tpu_custom_call", output_to_operand_aliasing={{0}: (3, {}), {1}: (4, {})} | custom-call | flops 1835008 | bytes 7340032 | tf_op jit(solution)/shard_map/finish/pallas_call | solution.py:98
  370.2 4.1 %finish.15 = (f32[2048,1792]{1,0:T(8,128)}, f32[2048,1792]{1,0:T(8,128)}) custom-call(s32[1]{0:T(128)} %bitcast.4.at, f32[256,1792]{1,0:T(8,128)} %collective-permute-done.17.refs_0_, f32[256,1792]{1,0:T(8,128)} %collective-permute-done.18.refs_1_, f32[2048,1792]{1,0:T(8,128)} %get-tuple-element.56.refs_2_, ...), custom_call_target="tpu_custom_call", output_to_operand_aliasing={{0}: (3, {}), {1}: (4, {})} | custom-call | flops 1835008 | bytes 7340032 | tf_op jit(solution)/shard_map/finish/pallas_call | solution.py:98
  374.3 4.1 %finish.16 = (f32[2048,1792]{1,0:T(8,128)}, f32[2048,1792]{1,0:T(8,128)}) custom-call(s32[1]{0:T(128)} %bitcast.3.at, f32[256,1792]{1,0:T(8,128)} %collective-permute-done.15.refs_0_, f32[256,1792]{1,0:T(8,128)} %collective-permute-done.16.refs_1_, f32[2048,1792]{1,0:T(8,128)} %get-tuple-element.58.refs_2_, ...), custom_call_target="tpu_custom_call", output_to_operand_aliasing={{0}: (3, {}), {1}: (4, {})} | custom-call | flops 1835008 | bytes 7340032 | tf_op jit(solution)/shard_map/finish/pallas_call | solution.py:98
  378.4 4.7 %finish.17 = (f32[2048,1792]{1,0:T(8,128)}, f32[2048,1792]{1,0:T(8,128)}) custom-call(s32[2]{0:T(128)} %pad_add_fusion.at, f32[256,1792]{1,0:T(8,128)} %collective-permute-done.refs_0_, f32[128,1792]{1,0:T(8,128)} %collective-permute-done.13.refs_1_, f32[256,1792]{1,0:T(8,128)} %collective-permute-done.7.refs_2_, ...), custom_call_target="tpu_custom_call", output_to_operand_aliasing={{0}: (5, {}), {1}: (6, {})} | custom-call | flops 917504 | bytes 7340032 | tf_op jit(solution)/shard_map/finish/pallas_call | solution.py:98
  383.1 3.4 finish.18
  (69 shorter events, 80.7 us)
Async XLA Ops:
  27.9 18.1 %collective-permute-start.25 = (f32[64,1792]{1,0:T(8,128)}, f32[64,1792]{1,0:T(8,128)}, u32[]{:S(2)}, u32[]{:S(2)}) collective-permute-start(f32[64,1792]{1,0:T(8,128)} %cut.16), channel_id=1, source_target_pairs={{0,7},{1,6},{2,5},{3,4},{4,3},{5,2},{6,1},{7,0},{8,15},{9,14},{10,... | collective-permute-start | bytes 1376264 | tf_op jit(solution)/shard_map/ppermute | solution.py:17
  29.7 22.0 %collective-permute-start.23 = (f32[64,1792]{1,0:T(8,128)}, f32[64,1792]{1,0:T(8,128)}, u32[]{:S(2)}, u32[]{:S(2)}) collective-permute-start(f32[64,1792]{1,0:T(8,128)} %cut.15), channel_id=1, source_target_pairs={{0,7},{1,6},{2,5},{3,4},{4,3},{5,2},{6,1},{7,0},{8,15},{9,14},{10,... | collective-permute-start | bytes 1376264 | tf_op jit(solution)/shard_map/ppermute | solution.py:17
  37.8 23.8 %collective-permute-start.26 = (f32[64,1792]{1,0:T(8,128)}, f32[64,1792]{1,0:T(8,128)}, u32[]{:S(2)}, u32[]{:S(2)}) collective-permute-start(f32[64,1792]{1,0:T(8,128)} %get-tuple-element.45), channel_id=1, source_target_pairs={{0,7},{1,6},{2,5},{3,4},{4,3},{5,2},{6,1},{7,0},{8,15},{9,14},{10,... | collective-permute-start | bytes 1376264 | tf_op jit(solution)/shard_map/ppermute | solution.py:17
  37.8 33.7 %collective-permute-start.24 = (f32[64,1792]{1,0:T(8,128)}, f32[64,1792]{1,0:T(8,128)}, u32[]{:S(2)}, u32[]{:S(2)}) collective-permute-start(f32[64,1792]{1,0:T(8,128)} %get-tuple-element.44), channel_id=1, source_target_pairs={{0,7},{1,6},{2,5},{3,4},{4,3},{5,2},{6,1},{7,0},{8,15},{9,14},{10,... | collective-permute-start | bytes 1376264 | tf_op jit(solution)/shard_map/ppermute | solution.py:17
  42.6 104.0 %collective-permute-start.21 = (f32[128,1792]{1,0:T(8,128)}, f32[128,1792]{1,0:T(8,128)}, u32[]{:S(2)}, u32[]{:S(2)}) collective-permute-start(f32[128,1792]{1,0:T(8,128)} %cut.14), channel_id=1, source_target_pairs={{0,7},{1,6},{2,5},{3,4},{4,3},{5,2},{6,1},{7,0},{8,15},{9,14},{10,... | collective-permute-start | bytes 2752520 | tf_op jit(solution)/shard_map/ppermute | solution.py:17
  46.0 103.2 %collective-permute-start.22 = (f32[128,1792]{1,0:T(8,128)}, f32[128,1792]{1,0:T(8,128)}, u32[]{:S(2)}, u32[]{:S(2)}) collective-permute-start(f32[128,1792]{1,0:T(8,128)} %get-tuple-element.43), channel_id=1, source_target_pairs={{0,7},{1,6},{2,5},{3,4},{4,3},{5,2},{6,1},{7,0},{8,15},{9,14},{10,... | collective-permute-start | bytes 2752520 | tf_op jit(solution)/shard_map/ppermute | solution.py:17
  51.7 97.5 %collective-permute-start.13 = (f32[128,1792]{1,0:T(8,128)}, f32[128,1792]{1,0:T(8,128)}, u32[]{:S(2)}, u32[]{:S(2)}) collective-permute-start(f32[128,1792]{1,0:T(8,128)} %get-tuple-element.41), channel_id=1, source_target_pairs={{0,2},{1,3},{2,0},{3,1},{4,6},{5,7},{6,4},{7,5},{8,10},{9,11},{10,... | collective-permute-start | bytes 2752520 | tf_op jit(solution)/shard_map/ppermute | solution.py:17
  61.6 91.1 %collective-permute-start.14 = (f32[128,1792]{1,0:T(8,128)}, f32[128,1792]{1,0:T(8,128)}, u32[]{:S(2)}, u32[]{:S(2)}) collective-permute-start(f32[128,1792]{1,0:T(8,128)} %get-tuple-element.42), channel_id=1, source_target_pairs={{0,4},{1,5},{2,6},{3,7},{4,0},{5,1},{6,2},{7,3},{8,12},{9,13},{10,... | collective-permute-start | bytes 2752520 | tf_op jit(solution)/shard_map/ppermute | solution.py:17
  71.5 65.0 %collective-permute-start.11 = (f32[64,1792]{1,0:T(8,128)}, f32[64,1792]{1,0:T(8,128)}, u32[]{:S(2)}, u32[]{:S(2)}) collective-permute-start(f32[64,1792]{1,0:T(8,128)} %get-tuple-element.39), channel_id=1, source_target_pairs={{0,2},{1,3},{2,0},{3,1},{4,6},{5,7},{6,4},{7,5},{8,10},{9,11},{10,... | collective-permute-start | bytes 1376264 | tf_op jit(solution)/shard_map/ppermute | solution.py:17
  136.5 20.8 %collective-permute-start.27 = (f32[256,1792]{1,0:T(8,128)}, f32[256,1792]{1,0:T(8,128)}, u32[]{:S(2)}, u32[]{:S(2)}) collective-permute-start(f32[256,1792]{1,0:T(8,128)} %cut.17), channel_id=1, source_target_pairs={{0,1},{1,0},{2,3},{3,2},{4,5},{5,4},{6,7},{7,6},{8,9},{9,8},{10,11... | collective-permute-start | bytes 5505032 | tf_op jit(solution)/shard_map/ppermute | solution.py:17
  146.6 44.1 %collective-permute-start.19 = (f32[256,1792]{1,0:T(8,128)}, f32[256,1792]{1,0:T(8,128)}, u32[]{:S(2)}, u32[]{:S(2)}) collective-permute-start(f32[256,1792]{1,0:T(8,128)} %cut.13), channel_id=1, source_target_pairs={{0,6},{1,7},{2,4},{3,5},{4,2},{5,3},{6,0},{7,1},{8,14},{9,15},{10,... | collective-permute-start | bytes 5505032 | tf_op jit(solution)/shard_map/ppermute | solution.py:17
  149.1 80.3 %collective-permute-start.17 = (f32[256,1792]{1,0:T(8,128)}, f32[256,1792]{1,0:T(8,128)}, u32[]{:S(2)}, u32[]{:S(2)}) collective-permute-start(f32[256,1792]{1,0:T(8,128)} %cut.12), channel_id=1, source_target_pairs={{0,5},{1,4},{2,7},{3,6},{4,1},{5,0},{6,3},{7,2},{8,13},{9,12},{10,... | collective-permute-start | bytes 5505032 | tf_op jit(solution)/shard_map/ppermute | solution.py:17
  149.2 81.9 %collective-permute-start.15 = (f32[256,1792]{1,0:T(8,128)}, f32[256,1792]{1,0:T(8,128)}, u32[]{:S(2)}, u32[]{:S(2)}) collective-permute-start(f32[256,1792]{1,0:T(8,128)} %cut.11), channel_id=1, source_target_pairs={{0,3},{1,2},{2,1},{3,0},{4,7},{5,6},{6,5},{7,4},{8,11},{9,10},{10,... | collective-permute-start | bytes 5505032 | tf_op jit(solution)/shard_map/ppermute | solution.py:17
  152.7 117.1 %collective-permute-start = (f32[256,1792]{1,0:T(8,128)}, f32[256,1792]{1,0:T(8,128)}, u32[]{:S(2)}, u32[]{:S(2)}) collective-permute-start(f32[256,1792]{1,0:T(8,128)} %cut.9), channel_id=1, source_target_pairs={{0,2},{1,3},{2,0},{3,1},{4,6},{5,7},{6,4},{7,5},{8,10},{9,11},{10,... | collective-permute-start | bytes 5505032 | tf_op jit(solution)/shard_map/ppermute | solution.py:17
  157.3 112.5 %collective-permute-start.7 = (f32[256,1792]{1,0:T(8,128)}, f32[256,1792]{1,0:T(8,128)}, u32[]{:S(2)}, u32[]{:S(2)}) collective-permute-start(f32[256,1792]{1,0:T(8,128)} %cut.10), channel_id=1, source_target_pairs={{0,4},{1,5},{2,6},{3,7},{4,0},{5,1},{6,2},{7,3},{8,12},{9,13},{10,... | collective-permute-start | bytes 5505032 | tf_op jit(solution)/shard_map/ppermute | solution.py:17
  190.7 80.4 %collective-permute-start.28 = (f32[256,1792]{1,0:T(8,128)}, f32[256,1792]{1,0:T(8,128)}, u32[]{:S(2)}, u32[]{:S(2)}) collective-permute-start(f32[256,1792]{1,0:T(8,128)} %calc.13), channel_id=1, source_target_pairs={{0,1},{1,0},{2,3},{3,2},{4,5},{5,4},{6,7},{7,6},{8,9},{9,8},{10,11... | collective-permute-start | bytes 5505032 | tf_op jit(solution)/shard_map/ppermute | solution.py:17
  229.4 79.3 %collective-permute-start.20 = (f32[256,1792]{1,0:T(8,128)}, f32[256,1792]{1,0:T(8,128)}, u32[]{:S(2)}, u32[]{:S(2)}) collective-permute-start(f32[256,1792]{1,0:T(8,128)} %calc.11), channel_id=1, source_target_pairs={{0,6},{1,7},{2,4},{3,5},{4,2},{5,3},{6,0},{7,1},{8,14},{9,15},{10,... | collective-permute-start | bytes 5505032 | tf_op jit(solution)/shard_map/ppermute | solution.py:17
  231.1 116.3 %collective-permute-start.18 = (f32[256,1792]{1,0:T(8,128)}, f32[256,1792]{1,0:T(8,128)}, u32[]{:S(2)}, u32[]{:S(2)}) collective-permute-start(f32[256,1792]{1,0:T(8,128)} %calc.10), channel_id=1, source_target_pairs={{0,5},{1,4},{2,7},{3,6},{4,1},{5,0},{6,3},{7,2},{8,13},{9,12},{10,... | collective-permute-start | bytes 5505032 | tf_op jit(solution)/shard_map/ppermute | solution.py:17
  269.8 79.1 %collective-permute-start.16 = (f32[256,1792]{1,0:T(8,128)}, f32[256,1792]{1,0:T(8,128)}, u32[]{:S(2)}, u32[]{:S(2)}) collective-permute-start(f32[256,1792]{1,0:T(8,128)} %calc.9), channel_id=1, source_target_pairs={{0,3},{1,2},{2,1},{3,0},{4,7},{5,6},{6,5},{7,4},{8,11},{9,10},{10,... | collective-permute-start | bytes 5505032 | tf_op jit(solution)/shard_map/ppermute | solution.py:17
  269.8 113.3 %collective-permute-start.12 = (f32[64,1792]{1,0:T(8,128)}, f32[64,1792]{1,0:T(8,128)}, u32[]{:S(2)}, u32[]{:S(2)}) collective-permute-start(f32[64,1792]{1,0:T(8,128)} %get-tuple-element.40), channel_id=1, source_target_pairs={{0,4},{1,5},{2,6},{3,7},{4,0},{5,1},{6,2},{7,3},{8,12},{9,13},{10,... | collective-permute-start | bytes 1376264 | tf_op jit(solution)/shard_map/ppermute | solution.py:17
  271.1 115.4 %collective-permute-start.10 = (f32[32,1792]{1,0:T(8,128)}, f32[32,1792]{1,0:T(8,128)}, u32[]{:S(2)}, u32[]{:S(2)}) collective-permute-start(f32[32,1792]{1,0:T(8,128)} %get-tuple-element.38), channel_id=1, source_target_pairs={{0,4},{1,5},{2,6},{3,7},{4,0},{5,1},{6,2},{7,3},{8,12},{9,13},{10,... | collective-permute-start | bytes 688136 | tf_op jit(solution)/shard_map/ppermute | solution.py:17
  308.8 77.8 %collective-permute-start.9 = (f32[32,1792]{1,0:T(8,128)}, f32[32,1792]{1,0:T(8,128)}, u32[]{:S(2)}, u32[]{:S(2)}) collective-permute-start(f32[32,1792]{1,0:T(8,128)} %get-tuple-element.37), channel_id=1, source_target_pairs={{0,2},{1,3},{2,0},{3,1},{4,6},{5,7},{6,4},{7,5},{8,10},{9,11},{10,... | collective-permute-start | bytes 688136 | tf_op jit(solution)/shard_map/ppermute | solution.py:17
  347.4 42.1 %collective-permute-start.6 = (f32[32,1792]{1,0:T(8,128)}, f32[32,1792]{1,0:T(8,128)}, u32[]{:S(2)}, u32[]{:S(2)}) collective-permute-start(f32[32,1792]{1,0:T(8,128)} %get-tuple-element.35), channel_id=1, source_target_pairs={{0,2},{1,3},{2,0},{3,1},{4,6},{5,7},{6,4},{7,5},{8,10},{9,11},{10,... | collective-permute-start | bytes 688136 | tf_op jit(solution)/shard_map/ppermute | solution.py:17
  348.9 40.7 %collective-permute-start.8 = (f32[32,1792]{1,0:T(8,128)}, f32[32,1792]{1,0:T(8,128)}, u32[]{:S(2)}, u32[]{:S(2)}) collective-permute-start(f32[32,1792]{1,0:T(8,128)} %get-tuple-element.36), channel_id=1, source_target_pairs={{0,4},{1,5},{2,6},{3,7},{4,0},{5,1},{6,2},{7,3},{8,12},{9,13},{10,... | collective-permute-start | bytes 688136 | tf_op jit(solution)/shard_map/ppermute | solution.py:17
  (5 other events, 22.3 us)
